TPU v7x, 32 devices: a whole 2x2x4 slice. The times are simulated.
32 devices in a mesh: dom: 8 (over y, x, core), feat: 4 (over z).
Axes of the slice: x: 2, y: 2, z: 4, core: 2. Of those that a mesh axis runs over, the one named last changes fastest.
Arguments:
- features: bfloat16 [512, 65536], P('feat', 'dom'), may hold values from -3 to 3
- send_blocks: int32 [8, 8, 8], P('dom'), may hold values from 0 to 63, as said below
- counts: int32 [8, 8], P('dom'), may hold values from 0 to 8, as said below
- tile_blocks: int32 [24, 512], P(None, 'dom'), may hold values from 0 to 127, as said below
- neighbours: int32 [24, 65536], P(None, 'dom'), may hold values from 0 to 127
- degree: int32 [65536], P('dom'), may hold values from 1 to 24
- epsilon: float32 [1], replicated, may hold values from -0.3 to 0.6
- w_first: bfloat16 [512, 512], replicated, may hold values from -0.25 to 0.25
- b_first: float32 [512], replicated, may hold values from -3 to 3
- w_second: bfloat16 [512, 512], replicated, may hold values from -0.25 to 0.25
- b_second: float32 [512], replicated, may hold values from -3 to 3
Outputs:
- updated: bfloat16 [65536, 512], P(('dom', 'feat'))
Inputs may be any that keep to these rules, and one draw needn't show every extreme that they name: `send_blocks`: entry [q, p, s] is a row block of partition q; the entries of one pair (q, p) are distinct. counts[q, p] leading slots of send_blocks[q, p] are used; zero where q == p; in every draw some partition receives 8 blocks from every other partition. `tile_blocks`: an entry for a row block of partition p is below 64 (a row block of p) or equals 64 + q * 8 + s for a slot s of a partition q other than p.
All inputs are finite; a program needn't handle non-finite values.
Results may differ from a plain program's by a relative error of at most 0.0055.
Values may be sent and summed in bfloat16 or wider, within the bound.
A program may use at most 64 MiB of HBM per device.

v0:
```python
import functools

import jax
import jax.numpy as jnp
from jax import lax
from jax.experimental import pallas as pl
from jax.experimental.pallas import tpu as pltpu
from jax.sharding import PartitionSpec as P

BLOCK = 128
SUBLANES = 16
SPLITS = 2
RAW = 8
PIECES = 4


def chunk_widths(cols):
    widths = []
    while sum(widths) < cols:
        widths.append(min(max(SUBLANES, sum(widths)), cols - sum(widths)))
    return widths


def kernel(
    parts, groups, pieces, widths,
    sb_hbm, cnt_hbm, tile_hbm, eps_ref, deg_hbm, b1_hbm, b2_hbm,
    feat_hbm, nbr_hbm, w1_hbm, w2_hbm,
    out_ref, parcel, w1_ref, w2_ref, b1_ref, b2_ref,
    *scratch,
):
    chunks = len(widths) - 1
    swap = chunks
    starts = [sum(widths[:c]) for c in range(chunks)]
    raw_start = sum(widths[:chunks])
    cols = raw_start + RAW
    count = len(widths)
    tables, locals_, stages, feats = (scratch[i * count:(i + 1) * count] for i in range(4))
    (sb_ref, cnt_ref, tile_ref, deg_ref, nbr_ref, zstage, zswap,
     hsend, hrecv, zsend, zrecv, zlast, raw_sem, in_sem) = scratch[4 * count:]
    me = lax.axis_index("dom")
    z = lax.axis_index("feat")
    slots = stages[0].shape[1]
    list_width, block_count = tile_ref.shape
    per_piece = block_count // groups // pieces
    piece_nodes = per_piece * BLOCK
    splits = zlast.shape[1]
    part_blocks = per_piece // splits
    part_nodes = part_blocks * BLOCK
    last = chunks - 1
    half = groups // 2
    partner = lax.rem(z + half, groups)

    def lanes(block):
        return pl.ds(pl.multiple_of(block * BLOCK, BLOCK), BLOCK)

    def halo_copy(c, peer, source):
        return pltpu.make_async_remote_copy(
            src_ref=stages[c].at[peer],
            dst_ref=tables[c].at[pl.ds(block_count + source * slots, slots)],
            send_sem=hsend.at[0],
            recv_sem=hrecv.at[c],
            device_id={"dom": peer},
            device_id_type=pl.DeviceIdType.MESH,
        )

    def parcel_rows(source, start, size):
        return pl.ds(pl.multiple_of(source * cols + start, RAW), size)

    def row_copy(c, p, dest):
        return pltpu.make_async_remote_copy(
            src_ref=zstage.at[p, dest, pl.ds(starts[c], widths[c])],
            dst_ref=parcel.at[p, parcel_rows(z, starts[c], widths[c])],
            send_sem=zsend.at[0],
            recv_sem=zrecv.at[p],
            device_id={"feat": dest},
            device_id_type=pl.DeviceIdType.MESH,
        )

    def part_lanes(h):
        return pl.ds(pl.multiple_of(h * part_nodes, BLOCK), part_nodes)

    def last_copy(p, h, dest):
        rows = pl.ds(starts[last], widths[last])
        return pltpu.make_async_remote_copy(
            src_ref=zstage.at[p, dest, rows, part_lanes(h)],
            dst_ref=parcel.at[p, parcel_rows(z, starts[last], widths[last]), part_lanes(h)],
            send_sem=zsend.at[0],
            recv_sem=zlast.at[p, h],
            device_id={"feat": dest},
            device_id_type=pl.DeviceIdType.MESH,
        )

    def swap_copy(p, i, part, owner):
        return pltpu.make_async_remote_copy(
            src_ref=zswap.at[p, i, pl.ds(part * RAW, RAW)],
            dst_ref=parcel.at[p, parcel_rows(owner, raw_start, RAW)],
            send_sem=zsend.at[0],
            recv_sem=zrecv.at[p],
            device_id={"feat": sibling(i)},
            device_id_type=pl.DeviceIdType.MESH,
        )

    def raw_copy():
        return pltpu.make_async_remote_copy(
            src_ref=feats[swap].at[pl.ds(0, RAW)],
            dst_ref=feats[swap].at[pl.ds(RAW, RAW)],
            send_sem=raw_sem.at[0],
            recv_sem=raw_sem.at[1],
            device_id={"feat": partner},
            device_id_type=pl.DeviceIdType.MESH,
        )

    def halo_all(c, sem):
        blocks = tables[c].at[pl.ds(0, (parts - 1) * slots)]
        return pltpu.make_async_copy(blocks, blocks, sem)

    def row_all(p, sem, dropped=0):
        rows = parcel.at[p, pl.ds(0, (groups - 1) * (cols - dropped) - RAW)]
        return pltpu.make_async_copy(rows, rows, sem)

    def last_all(p, h):
        rows = parcel.at[p, pl.ds(0, (groups - 1) * widths[last]), part_lanes(h)]
        return pltpu.make_async_copy(rows, rows, zlast.at[p, h])

    def sibling(i):
        return (z // half) * half + lax.rem(lax.rem(z, half) + i, half)

    def dest_of(k):
        if k < half:
            lower = z // half
            return lower * k + (1 - lower) * (groups - 1 - k)
        return sibling(k - half + 1)

    barrier = pltpu.get_barrier_semaphore()

    @pl.loop(1, groups)
    def _(k):
        pl.semaphore_signal(
            barrier, inc=1, device_id={"feat": lax.rem(z + k, groups)},
            device_id_type=pl.DeviceIdType.MESH,
        )

    @pl.loop(1, parts)
    def _(k):
        pl.semaphore_signal(
            barrier, inc=1, device_id={"dom": lax.rem(me + k, parts)},
            device_id_type=pl.DeviceIdType.MESH,
        )

    loads = [
        pltpu.make_async_copy(
            feat_hbm.at[pl.ds(starts[c], widths[c])], feats[c], in_sem.at[c]
        )
        for c in range(chunks)
    ]
    raw_load = pltpu.make_async_copy(
        feat_hbm.at[pl.ds(raw_start, RAW)], feats[swap].at[pl.ds(0, RAW)], in_sem.at[swap]
    )
    small = [
        pltpu.make_async_copy(source, target, in_sem.at[count])
        for source, target in ((sb_hbm, sb_ref), (cnt_hbm, cnt_ref))
    ]
    lists = [
        pltpu.make_async_copy(source, target, in_sem.at[count + 1])
        for source, target in ((tile_hbm, tile_ref), (deg_hbm, deg_ref), (nbr_hbm, nbr_ref))
    ]
    weights = [
        pltpu.make_async_copy(source, target, in_sem.at[count + 2])
        for source, target in (
            (w1_hbm, w1_ref), (w2_hbm, w2_ref), (b1_hbm, b1_ref), (b2_hbm, b2_ref),
        )
    ]
    for load in loads[:1] + small + [raw_load] + loads[1:] + lists + weights:
        load.start()

    def lay_out(c):
        @pl.loop(0, block_count, unroll=4)
        def _(b):
            block = feats[c][:, lanes(b)]
            locals_[c][b] = block
            tables[c][b] = block

        tables[c][pl.ds(block_count + me * slots, slots)] = jnp.zeros(
            (slots, widths[c], BLOCK), jnp.bfloat16
        )

    def fill(c, peer):
        for s in range(slots):
            used = (s < cnt_ref[0, peer]).astype(jnp.float32)
            block = locals_[c][sb_ref[0, peer, s]]
            stages[c][peer, s] = (block.astype(jnp.float32) * used).astype(jnp.bfloat16)

    def send_halo(c):
        @pl.loop(1, parts)
        def _(k):
            peer = lax.rem(me + k, parts)
            fill(c, peer)
            halo_copy(c, peer, me).start()

    loads[0].wait()
    lay_out(0)
    for load in small:
        load.wait()

    @pl.loop(1, parts)
    def _(k):
        fill(0, lax.rem(me + k, parts))

    raw_load.wait()
    pl.semaphore_wait(barrier, parts + groups - 2)

    raw_copy().start()

    @pl.loop(1, parts)
    def _(k):
        halo_copy(0, lax.rem(me + k, parts), me).start()

    for c in range(1, chunks):
        loads[c].wait()
        lay_out(c)
        send_halo(c)

    for load in lists:
        load.wait()
    gain = 1.0 + eps_ref[0]

    lane_gather = lax.GatherDimensionNumbers(
        offset_dims=(), collapsed_slice_dims=(1,), start_index_map=(1,),
        operand_batching_dims=(0,), start_indices_batching_dims=(0,),
    )

    def mixed_block(c, b):
        shape = (widths[c], BLOCK)
        total = gain * feats[c][:, lanes(b)].astype(jnp.float32)
        near = jnp.zeros(shape, jnp.float32)
        degree = jnp.broadcast_to(deg_ref[pl.ds(b, 1), :], shape)
        for j in range(list_width):
            tile = tables[c][tile_ref[j, b]].astype(jnp.float32)
            index = jnp.broadcast_to(nbr_ref[pl.ds(j, 1), lanes(b)], shape)
            taken = lax.gather(
                tile, index[..., None], lane_gather, slice_sizes=(1, 1),
                mode=lax.GatherScatterMode.PROMISE_IN_BOUNDS,
            )
            near = near + jnp.where(degree > j, taken, 0.0)
        return (total + near).astype(jnp.bfloat16)

    def blocks_of(c, p, dest, store):
        first = (dest * pieces + p) * per_piece
        unroll = per_piece if widths[c] <= 2 * SUBLANES else max(per_piece // 2, 1)

        @pl.loop(0, per_piece, unroll=unroll)
        def _(i):
            store(i, mixed_block(c, first + i))

    def aggregate(c, p, k):
        dest = dest_of(k) if k < groups - 1 else z

        def store(i, block):
            if k < groups - 1:
                zstage[p, dest, pl.ds(starts[c], widths[c]), lanes(i)] = block
            else:
                parcel[p, parcel_rows(z, starts[c], widths[c]), lanes(i)] = block

        blocks_of(c, p, dest, store)
        if k < groups - 1:
            row_copy(c, p, dest).start()

    def aggregate_swap(p, i):
        def store(n, block):
            if i > 0:
                zswap[p, i, :, lanes(n)] = block
            else:
                parcel[p, parcel_rows(z, raw_start, RAW), lanes(n)] = block[:RAW]
                parcel[p, parcel_rows(partner, raw_start, RAW), lanes(n)] = block[RAW:]

        blocks_of(swap, p, sibling(i), store)
        if i > 0:
            swap_copy(p, i, 0, z).start()
            swap_copy(p, i, 1, partner).start()

    def aggregate_last(p, k):
        dest = dest_of(k) if k < groups - 1 else z
        first = (dest * pieces + p) * per_piece
        rows = pl.ds(starts[last], widths[last])

        @pl.loop(0, splits)
        def _(h):
            for n in range(part_blocks):
                i = h * part_blocks + n
                block = mixed_block(last, first + i)
                if k < groups - 1:
                    zstage[p, dest, rows, lanes(i)] = block
                else:
                    parcel[p, parcel_rows(z, starts[last], widths[last]), lanes(i)] = block
            if k < groups - 1:
                last_copy(p, h, dest).start()

    def run(c, ks):
        @pl.loop(0, pieces)
        def _(p):
            for k in ks:
                aggregate(c, p, k)

    def run_ending(ks):
        for k in ks:
            @pl.loop(pieces - ending, pieces)
            def _(p):
                aggregate_last(p, k)

    across, within = range(half), range(half, groups)
    ending = pieces // 2
    for c in range(chunks):
        halo_all(c, hrecv.at[c]).wait()
        if c == chunks - 1:
            halo_all(swap, hrecv.at[swap]).wait()

            @pl.loop(0, pieces - ending)
            def _(p):
                for k in range(groups):
                    aggregate_last(p, k)
                for i in reversed(range(half)):
                    aggregate_swap(p, i)

            run_ending(across[:half // 2])

            @pl.loop(pieces - ending, pieces)
            def _(p):
                for k in within[:-1]:
                    aggregate_last(p, k)
                for i in reversed(range(half)):
                    aggregate_swap(p, i)

            run_ending(across[half // 2:])
            run_ending(within[-1:])
        else:
            run(c, across)
        if c == min(1, chunks - 2):
            raw_copy().wait()
            lay_out(swap)
            send_halo(swap)
        if 0 < c < chunks - 1:
            run(c - 1, within)
        if c == chunks - 2:
            run(c, within)

    for load in weights:
        load.wait()
    for c in range(count):
        halo_all(c, hsend.at[0]).wait()

    def finish(p, h):
        last_all(p, h).wait()
        first = pl.multiple_of((p * splits + h) * part_nodes, part_nodes)
        out_ref[pl.ds(first, part_nodes), :] = network(
            parcel[p, :, part_lanes(h)], w1_ref, w2_ref, b1_ref, b2_ref
        )

    @pl.loop(0, pieces - 1)
    def _(p):
        row_all(p, zrecv.at[p], widths[last]).wait()

        @pl.loop(0, splits)
        def _(h):
            finish(p, h)

    final = pieces - 1
    row_all(final, zrecv.at[final], widths[last]).wait()
    for p in range(final):
        row_all(p, zsend.at[0]).wait()
    for h in range(splits - 1):
        finish(final, h)
    last_all(final, splits - 1).wait()
    row_all(final, zsend.at[0]).wait()


def network(columns, w1_ref, w2_ref, b1_ref, b2_ref):
    hidden = lax.dot_general(
        columns, w1_ref[...], (((0,), (0,)), ((), ())), preferred_element_type=jnp.float32
    ) + b1_ref[...]
    hidden = jnp.maximum(hidden, 0.0).astype(jnp.bfloat16)
    return (
        jnp.dot(hidden, w2_ref[...], preferred_element_type=jnp.float32) + b2_ref[...]
    ).astype(jnp.bfloat16)


def closing_kernel(
    part_nodes, out_ref, parcel, w1_ref, w2_ref, b1_ref, b2_ref, result_hbm, rest_ref, sems
):
    done = out_ref.shape[0] - part_nodes
    pieces, _, piece_nodes = parcel.shape
    early = pltpu.make_async_copy(
        out_ref.at[pl.ds(0, done)], result_hbm.at[pl.ds(0, done)], sems.at[0]
    )
    early.start()
    columns = parcel[pieces - 1, :, pl.ds(piece_nodes - part_nodes, part_nodes)]
    rest_ref[...] = network(columns, w1_ref, w2_ref, b1_ref, b2_ref)
    late = pltpu.make_async_copy(
        rest_ref, result_hbm.at[pl.ds(done, part_nodes)], sems.at[1]
    )
    late.start()
    early.wait()
    late.wait()


def in_hbm(array):
    return pltpu.with_memory_space_constraint(array, pltpu.HBM)


def per_device(
    features, send_blocks, counts, tile_blocks, neighbours, degree, epsilon,
    w_first, b_first, w_second, b_second,
):
    parts = lax.axis_size("dom")
    groups = lax.axis_size("feat")
    cols, rows = features.shape
    slots = send_blocks.shape[2]
    widths = chunk_widths(cols - RAW) + [2 * RAW]
    count = len(widths)
    block_count = rows // BLOCK
    owned = rows // groups
    pieces = min(PIECES, owned // BLOCK)
    splits = SPLITS if (owned // BLOCK // pieces) % SPLITS == 0 else 1
    hidden_cols, out_cols = w_second.shape
    depth = w_first.shape[0]
    hbm = pl.BlockSpec(memory_space=pltpu.HBM)
    smem = pl.BlockSpec(memory_space=pltpu.SMEM)
    bf16 = jnp.bfloat16
    vmem = pl.BlockSpec(memory_space=pltpu.VMEM)
    part_nodes = owned // pieces // splits
    handed = pl.pallas_call(
        functools.partial(kernel, parts, groups, pieces, widths),
        out_shape=(
            pltpu.VMEM((owned, out_cols), bf16),
            pltpu.VMEM((pieces, depth, owned // pieces), bf16),
            pltpu.VMEM((depth, hidden_cols), bf16),
            pltpu.VMEM((hidden_cols, out_cols), bf16),
            pltpu.VMEM((1, hidden_cols), jnp.float32),
            pltpu.VMEM((1, out_cols), jnp.float32),
        ),
        in_specs=[hbm] * 3 + [smem] + [hbm] * 7,
        out_specs=(vmem,) * 6,
        scratch_shapes=[
            pltpu.VMEM((block_count + parts * slots, w, BLOCK), bf16) for w in widths
        ] + [
            pltpu.VMEM((block_count, w, BLOCK), bf16) for w in widths
        ] + [
            pltpu.VMEM((parts, slots, w, BLOCK), bf16) for w in widths
        ] + [
            pltpu.VMEM((w, rows), bf16) for w in widths
        ] + [
            pltpu.SMEM(send_blocks.shape, jnp.int32),
            pltpu.SMEM(counts.shape, jnp.int32),
            pltpu.SMEM(tile_blocks.shape, jnp.int32),
            pltpu.VMEM((block_count, BLOCK), jnp.int32),
            pltpu.VMEM(neighbours.shape, jnp.int32),
            pltpu.VMEM((pieces, groups, cols, owned // pieces), bf16),
            pltpu.VMEM((pieces, groups // 2, 2 * RAW, owned // pieces), bf16),
            pltpu.SemaphoreType.DMA((1,)),
            pltpu.SemaphoreType.DMA((count,)),
            pltpu.SemaphoreType.DMA((1,)),
            pltpu.SemaphoreType.DMA((pieces,)),
            pltpu.SemaphoreType.DMA((pieces, splits)),
            pltpu.SemaphoreType.DMA((2,)),
            pltpu.SemaphoreType.DMA((count + 3,)),
        ],
        compiler_params=pltpu.CompilerParams(
            collective_id=0, has_side_effects=True, vmem_limit_bytes=48 * 1024 * 1024
        ),
    )(
        in_hbm(send_blocks), in_hbm(counts), in_hbm(tile_blocks), epsilon,
        in_hbm(degree.reshape(block_count, BLOCK)),
        in_hbm(b_first.reshape(1, -1)), in_hbm(b_second.reshape(1, -1)),
        in_hbm(features), in_hbm(neighbours), in_hbm(w_first), in_hbm(w_second),
    )
    return pl.pallas_call(
        functools.partial(closing_kernel, part_nodes),
        out_shape=jax.ShapeDtypeStruct((owned, out_cols), bf16),
        in_specs=[vmem] * 6,
        out_specs=hbm,
        scratch_shapes=[
            pltpu.VMEM((part_nodes, out_cols), bf16), pltpu.SemaphoreType.DMA((2,)),
        ],
        compiler_params=pltpu.CompilerParams(vmem_limit_bytes=16 * 1024 * 1024),
    )(*handed)


def solution(mesh):
    return jax.shard_map(
        per_device,
        mesh=mesh,
        in_specs=(
            P("feat", "dom"),
            P("dom", None, None),
            P("dom", None),
            P(None, "dom"),
            P(None, "dom"),
            P("dom"),
            P(), P(), P(), P(), P(),
        ),
        out_specs=P(("dom", "feat"), None),
        check_vma=False,
    )
```

profile of v0, /device:TPU:0, one launch (start us, length us, event | category | flops | bytes accessed | tf_op | source)
XLA Modules:
  0.0 55.0 jit_solution(6235744175962450466)
XLA Ops:
  0.7 52.9 %shard_map.109 = (bf16[2048,512]{1,0:T(8,128)(2,1)S(1)}, bf16[4,512,512]{2,1,0:T(8,128)(2,1)S(1)}, bf16[512,512]{1,0:T(8,128)(2,1)S(1)}, bf16[512,512]{1,0:T(8,1...) custom-call(s32[1,8,8]{2,1,0:T(8,128)} %sb_hbm.1, s32[1,8]{1,0:T(1,128)} %cnt_hbm.1, s32[24,64]{1,0:T(8,128)} %tile_hbm.1, ...), custom_call_target="tpu_custom_call" | custom-call | tf_op jit(solution)/shard_map/pallas_call | solution.py:430
  53.6 1.4 %shard_map.110 = bf16[2048,512]{1,0:T(8,128)(2,1)} custom-call(bf16[2048,512]{1,0:T(8,128)(2,1)S(1)} %get-tuple-element.11.out_ref, bf16[4,512,512]{2,1,0:T(8,128)(2,1)S(1)} %get-tuple-element.12.parcel, bf16[512,512]{1,0:T(8,128)(2,1)S(1)} %get-tuple-element.13.w1_ref, bf16[512,512]{1,0:T(8,128)(2,1)S(1)} %get-tuple-element.14.w2_ref, ...), custom_call_target="tpu_custom_call" | custom-call | tf_op jit(solution)/shard_map/pallas_call | solution.py:475
where the time goes:
time: 55.8 us; the launch traced here: 55 us
  Pallas kernels  54.3 us (97%)
  between operations  0.66 us (1%)
    pallas_call x1, Pallas kernels, per_device(): pl.pallas_call(functools.partial(kernel, parts, groups, pieces, widths),...  52.9 us
    pallas_call x1, Pallas kernels, per_device(): pl.pallas_call(functools.partial(closing_kernel, part_nodes), out_shape=j...  1.39 us

commit v1 on v0

--- a/solution.py
+++ b/solution.py
@@ -48,7 +48,7 @@
     part_nodes = part_blocks * BLOCK
     last = chunks - 1
     half = groups // 2
-    partner = lax.rem(z + half, groups)
+    partner = groups - 1 - z
 
     def lanes(block):
         return pl.ds(pl.multiple_of(block * BLOCK, BLOCK), BLOCK)
@@ -131,19 +131,23 @@
             return lower * k + (1 - lower) * (groups - 1 - k)
         return sibling(k - half + 1)
 
+    def peer_of(k):
+        peer, bit = 0, 1
+        while bit < parts:
+            peer = peer + lax.rem(me // bit + k // bit, 2) * bit
+            bit *= 2
+        return peer
+
     barrier = pltpu.get_barrier_semaphore()
 
-    @pl.loop(1, groups)
-    def _(k):
+    for k in range(1, groups):
         pl.semaphore_signal(
             barrier, inc=1, device_id={"feat": lax.rem(z + k, groups)},
             device_id_type=pl.DeviceIdType.MESH,
         )
-
-    @pl.loop(1, parts)
-    def _(k):
+    for k in reversed(range(1, parts)):
         pl.semaphore_signal(
-            barrier, inc=1, device_id={"dom": lax.rem(me + k, parts)},
+            barrier, inc=1, device_id={"dom": peer_of(k)},
             device_id_type=pl.DeviceIdType.MESH,
         )
 
@@ -193,7 +197,7 @@
     def send_halo(c):
         @pl.loop(1, parts)
         def _(k):
-            peer = lax.rem(me + k, parts)
+            peer = peer_of(parts - k)
             fill(c, peer)
             halo_copy(c, peer, me).start()
 
@@ -211,9 +215,8 @@
 
     raw_copy().start()
 
-    @pl.loop(1, parts)
-    def _(k):
-        halo_copy(0, lax.rem(me + k, parts), me).start()
+    for k in reversed(range(1, parts)):
+        halo_copy(0, peer_of(k), me).start()
 
     for c in range(1, chunks):
         loads[c].wait()

time: 55.8 us -> 55.9 us (level); the launches traced: 55 us -> 55.7 us
  Pallas kernels: 54.3 us -> 55.1 us
    pallas_call x1, Pallas kernels: 52.9 us -> 53.7 us  [per_device(): pl.pallas_call(functools.partial(kernel, parts, groups, pieces, widths),...]
where the time goes in v1:
time: 55.9 us; the launch traced here: 55.7 us
  Pallas kernels  55.1 us (99%)
  between operations  0.66 us (1%)
    pallas_call x1, Pallas kernels, per_device(): pl.pallas_call(functools.partial(kernel, parts, groups, pieces, widths),...  53.7 us
    pallas_call x1, Pallas kernels, per_device(): pl.pallas_call(functools.partial(closing_kernel, part_nodes), out_shape=j...  1.39 us

profile of v1, /device:TPU:0, one launch (start us, length us, event | category | flops | bytes accessed | tf_op | source)
XLA Modules:
  0.0 55.7 jit_solution(8602600285694434627)
XLA Ops:
  0.7 53.7 %shard_map.109 = (bf16[2048,512]{1,0:T(8,128)(2,1)S(1)}, bf16[4,512,512]{2,1,0:T(8,128)(2,1)S(1)}, bf16[512,512]{1,0:T(8,128)(2,1)S(1)}, bf16[512,512]{1,0:T(8,1...) custom-call(s32[1,8,8]{2,1,0:T(8,128)} %sb_hbm.1, s32[1,8]{1,0:T(1,128)} %cnt_hbm.1, s32[24,64]{1,0:T(8,128)} %tile_hbm.1, ...), custom_call_target="tpu_custom_call" | custom-call | tf_op jit(solution)/shard_map/pallas_call | solution.py:433
  54.3 1.4 %shard_map.110 = bf16[2048,512]{1,0:T(8,128)(2,1)} custom-call(bf16[2048,512]{1,0:T(8,128)(2,1)S(1)} %get-tuple-element.11.out_ref, bf16[4,512,512]{2,1,0:T(8,128)(2,1)S(1)} %get-tuple-element.12.parcel, bf16[512,512]{1,0:T(8,128)(2,1)S(1)} %get-tuple-element.13.w1_ref, bf16[512,512]{1,0:T(8,128)(2,1)S(1)} %get-tuple-element.14.w2_ref, ...), custom_call_target="tpu_custom_call" | custom-call | tf_op jit(solution)/shard_map/pallas_call | solution.py:478

commit v2 on v1

--- a/solution.py
+++ b/solution.py
@@ -43,12 +43,14 @@
     list_width, block_count = tile_ref.shape
     per_piece = block_count // groups // pieces
     piece_nodes = per_piece * BLOCK
-    splits = zlast.shape[1]
+    splits = zlast.shape[0]
+    final = pieces - 1
     part_blocks = per_piece // splits
     part_nodes = part_blocks * BLOCK
+    group = max(per_piece // 2, part_blocks)
     last = chunks - 1
     half = groups // 2
-    partner = groups - 1 - z
+    partner = lax.rem(z + half, groups)
 
     def lanes(block):
         return pl.ds(pl.multiple_of(block * BLOCK, BLOCK), BLOCK)
@@ -79,13 +81,13 @@
     def part_lanes(h):
         return pl.ds(pl.multiple_of(h * part_nodes, BLOCK), part_nodes)
 
-    def last_copy(p, h, dest):
+    def last_copy(p, dest, nodes, sem):
         rows = pl.ds(starts[last], widths[last])
         return pltpu.make_async_remote_copy(
-            src_ref=zstage.at[p, dest, rows, part_lanes(h)],
-            dst_ref=parcel.at[p, parcel_rows(z, starts[last], widths[last]), part_lanes(h)],
+            src_ref=zstage.at[p, dest, rows, nodes],
+            dst_ref=parcel.at[p, parcel_rows(z, starts[last], widths[last]), nodes],
             send_sem=zsend.at[0],
-            recv_sem=zlast.at[p, h],
+            recv_sem=sem,
             device_id={"feat": dest},
             device_id_type=pl.DeviceIdType.MESH,
         )
@@ -118,9 +120,9 @@
         rows = parcel.at[p, pl.ds(0, (groups - 1) * (cols - dropped) - RAW)]
         return pltpu.make_async_copy(rows, rows, sem)
 
-    def last_all(p, h):
-        rows = parcel.at[p, pl.ds(0, (groups - 1) * widths[last]), part_lanes(h)]
-        return pltpu.make_async_copy(rows, rows, zlast.at[p, h])
+    def last_all(h):
+        rows = parcel.at[final, pl.ds(0, (groups - 1) * widths[last]), part_lanes(h)]
+        return pltpu.make_async_copy(rows, rows, zlast.at[h])
 
     def sibling(i):
         return (z // half) * half + lax.rem(lax.rem(z, half) + i, half)
@@ -283,20 +285,25 @@
 
     def aggregate_last(p, k):
         dest = dest_of(k) if k < groups - 1 else z
-        first = (dest * pieces + p) * per_piece
-        rows = pl.ds(starts[last], widths[last])
-
-        @pl.loop(0, splits)
-        def _(h):
-            for n in range(part_blocks):
-                i = h * part_blocks + n
-                block = mixed_block(last, first + i)
-                if k < groups - 1:
-                    zstage[p, dest, rows, lanes(i)] = block
-                else:
-                    parcel[p, parcel_rows(z, starts[last], widths[last]), lanes(i)] = block
+
+        def block_of(i):
+            block = mixed_block(last, (dest * pieces + p) * per_piece + i)
             if k < groups - 1:
-                last_copy(p, h, dest).start()
+                zstage[p, dest, pl.ds(starts[last], widths[last]), lanes(i)] = block
+            else:
+                parcel[p, parcel_rows(z, starts[last], widths[last]), lanes(i)] = block
+
+        @pl.loop(0, per_piece // group)
+        def _(g):
+            for n in range(group):
+                block_of(g * group + n)
+            if k < groups - 1 and p is final:
+                for h in range(group // part_blocks):
+                    part = g * (group // part_blocks) + h
+                    last_copy(p, dest, part_lanes(part), zlast.at[part]).start()
+
+        if k < groups - 1 and p is not final:
+            last_copy(p, dest, pl.ds(0, piece_nodes), zrecv.at[p]).start()
 
     def run(c, ks):
         @pl.loop(0, pieces)
@@ -306,9 +313,11 @@
 
     def run_ending(ks):
         for k in ks:
-            @pl.loop(pieces - ending, pieces)
+            @pl.loop(pieces - ending, final)
             def _(p):
                 aggregate_last(p, k)
+
+            aggregate_last(final, k)
 
     across, within = range(half), range(half, groups)
     ending = pieces // 2
@@ -326,10 +335,10 @@
 
             run_ending(across[:half // 2])
 
+            run_ending(within[:-1])
+
             @pl.loop(pieces - ending, pieces)
             def _(p):
-                for k in within[:-1]:
-                    aggregate_last(p, k)
                 for i in reversed(range(half)):
                     aggregate_swap(p, i)
 
@@ -351,28 +360,24 @@
     for c in range(count):
         halo_all(c, hsend.at[0]).wait()
 
-    def finish(p, h):
-        last_all(p, h).wait()
-        first = pl.multiple_of((p * splits + h) * part_nodes, part_nodes)
-        out_ref[pl.ds(first, part_nodes), :] = network(
-            parcel[p, :, part_lanes(h)], w1_ref, w2_ref, b1_ref, b2_ref
-        )
-
-    @pl.loop(0, pieces - 1)
+    def finish(p, first, nodes):
+        row = pl.multiple_of(p * piece_nodes + first, nodes)
+        out_ref[pl.ds(row, nodes), :] = network(
+            parcel[p, :, pl.ds(first, nodes)], w1_ref, w2_ref, b1_ref, b2_ref
+        )
+
+    @pl.loop(0, final)
     def _(p):
-        row_all(p, zrecv.at[p], widths[last]).wait()
-
-        @pl.loop(0, splits)
-        def _(h):
-            finish(p, h)
-
-    final = pieces - 1
+        row_all(p, zrecv.at[p]).wait()
+        finish(p, 0, piece_nodes)
+
     row_all(final, zrecv.at[final], widths[last]).wait()
     for p in range(final):
         row_all(p, zsend.at[0]).wait()
     for h in range(splits - 1):
-        finish(final, h)
-    last_all(final, splits - 1).wait()
+        last_all(h).wait()
+        finish(final, h * part_nodes, part_nodes)
+    last_all(splits - 1).wait()
     row_all(final, zsend.at[0]).wait()
 
 
@@ -422,7 +427,7 @@
     block_count = rows // BLOCK
     owned = rows // groups
     pieces = min(PIECES, owned // BLOCK)
-    splits = SPLITS if (owned // BLOCK // pieces) % SPLITS == 0 else 1
+    splits = min(SPLITS, owned // BLOCK // pieces)
     hidden_cols, out_cols = w_second.shape
     depth = w_first.shape[0]
     hbm = pl.BlockSpec(memory_space=pltpu.HBM)
@@ -462,7 +467,7 @@
             pltpu.SemaphoreType.DMA((count,)),
             pltpu.SemaphoreType.DMA((1,)),
             pltpu.SemaphoreType.DMA((pieces,)),
-            pltpu.SemaphoreType.DMA((pieces, splits)),
+            pltpu.SemaphoreType.DMA((splits,)),
             pltpu.SemaphoreType.DMA((2,)),
             pltpu.SemaphoreType.DMA((count + 3,)),
         ],

time: 55.9 us -> 55.9 us (level)
  no operation moved by 1% of the time
where the time goes in v2:
time: 55.9 us; the launch traced here: 55.7 us
  Pallas kernels  55.1 us (99%)
  between operations  0.66 us (1%)
    pallas_call x1, Pallas kernels, per_device(): pl.pallas_call(functools.partial(kernel, parts, groups, pieces, widths),...  53.7 us
    pallas_call x1, Pallas kernels, per_device(): pl.pallas_call(functools.partial(closing_kernel, part_nodes), out_shape=j...  1.39 us

profile of v2, /device:TPU:0, one launch (start us, length us, event | category | flops | bytes accessed | tf_op | source)
XLA Modules:
  0.0 55.7 jit_solution(6680269862743826329)
XLA Ops:
  0.7 53.7 %shard_map.109 = (bf16[2048,512]{1,0:T(8,128)(2,1)S(1)}, bf16[4,512,512]{2,1,0:T(8,128)(2,1)S(1)}, bf16[512,512]{1,0:T(8,128)(2,1)S(1)}, bf16[512,512]{1,0:T(8,1...) custom-call(s32[1,8,8]{2,1,0:T(8,128)} %sb_hbm.1, s32[1,8]{1,0:T(1,128)} %cnt_hbm.1, s32[24,64]{1,0:T(8,128)} %tile_hbm.1, ...), custom_call_target="tpu_custom_call" | custom-call | tf_op jit(solution)/shard_map/pallas_call | solution.py:438
  54.3 1.4 %shard_map.110 = bf16[2048,512]{1,0:T(8,128)(2,1)} custom-call(bf16[2048,512]{1,0:T(8,128)(2,1)S(1)} %get-tuple-element.11.out_ref, bf16[4,512,512]{2,1,0:T(8,128)(2,1)S(1)} %get-tuple-element.12.parcel, bf16[512,512]{1,0:T(8,128)(2,1)S(1)} %get-tuple-element.13.w1_ref, bf16[512,512]{1,0:T(8,128)(2,1)S(1)} %get-tuple-element.14.w2_ref, ...), custom_call_target="tpu_custom_call" | custom-call | tf_op jit(solution)/shard_map/pallas_call | solution.py:483
